TPU v7x, 256 devices: a whole 4x4x8 slice. The times are simulated.
256 devices in a mesh: blk: 32 (over x, z), src: 2 (over y_lo), layer: 4 (over y_hi, core).
Axes of the slice: x: 4, y: 4 (y_hi: 2, y_lo: 2; y = y_hi * 2 + y_lo), z: 8, core: 2. Of those that a mesh axis runs over, the one named last changes fastest.
Arguments:
- resident_act: bfloat16 [4, 16384, 4096], P('layer', 'blk'), may hold values from -6 to 6
- resident_grad: bfloat16 [4, 16384, 4096], P('layer', 'blk'), may hold values from -6 to 6
- source_act: bfloat16 [4, 1024, 4096], P('layer', ('blk', 'src')), may hold values from -6 to 6
- source_grad: bfloat16 [4, 1024, 4096], P('layer', ('blk', 'src')), may hold values from -6 to 6
- probes: bfloat16 [1024, 256], P(('blk', 'src')), may hold values from -6 to 6
Outputs:
- kernel_product: float32 [16384, 256], P(('blk', 'layer'))
All inputs are finite; a program needn't handle non-finite values.
Results may differ from a plain program's by a relative error of at most 0.0029.
Values may be sent and summed in bfloat16 or wider, within the bound.
No kernel may reach another device: no remote copies, remote signals or barrier semaphores. Data moves between devices by JAX's collectives and lax.ppermute only.
A program may use at most 64 MiB of HBM per device.

v0:
```python
import jax
import jax.numpy as jnp
from jax import lax
from jax.sharding import PartitionSpec as P

LAYERS = 4


def contract_rows(left, right):
    return lax.dot_general(
        left, right, (((1,), (1,)), ((), ())), preferred_element_type=jnp.float32
    )


def on_device(resident_act, resident_grad, source_act, source_grad, probes):
    width = resident_act.shape[2]
    blocks = lax.axis_size("blk")
    source_total = source_act.shape[1] * blocks * lax.axis_size("src")
    inverse_width = jnp.float32(1.0 / width)
    probe_rows = lax.all_gather(probes, "blk", axis=0, tiled=True)
    acts = lax.all_gather(source_act[0], "blk", axis=0, tiled=True)
    grads = lax.all_gather(source_grad[0], "blk", axis=0, tiled=True)
    act_gram = contract_rows(acts, resident_act[0])
    grad_gram = contract_rows(grads, resident_grad[0])
    kernel = (act_gram * grad_gram * inverse_width).astype(jnp.bfloat16)
    total = lax.dot_general(
        kernel, probe_rows, (((0,), (0,)), ((), ())), preferred_element_type=jnp.float32
    )
    part = lax.psum_scatter(total, "layer", scatter_dimension=0, tiled=True)
    result = lax.psum(part, "src")
    return result * jnp.float32((LAYERS * source_total) ** (-0.5))


def solution(mesh):
    in_specs = (
        P("layer", "blk", None),
        P("layer", "blk", None),
        P("layer", ("blk", "src"), None),
        P("layer", ("blk", "src"), None),
        P(("blk", "src"), None),
    )
    out_specs = P(("blk", "layer"), None)
    return jax.shard_map(
        on_device, mesh=mesh, in_specs=in_specs, out_specs=out_specs, check_vma=False
    )
```

profile of v0, /device:TPU:1, one launch (start us, length us, event | category | flops | bytes accessed | tf_op | source)
XLA Modules:
  0.0 257.1 jit_solution(9820898550968278613)
XLA Ops:
  6.5 0.0 all-gather.7.cloned.1.call-start
  6.5 0.7 all-gather.7.cloned.1.call-update
  7.3 0.0 all-gather.5.cloned.1.call-start
  7.3 0.7 all-gather.5.cloned.1.call-update
  8.0 0.0 reduce-scatter.2.cloned.1.call-start
  8.1 42.0 %all_gather.11 = bf16[512,256]{1,0:T(8,128)(2,1)S(1)} all-gather(bf16[16,256]{1,0:T(8,128)(2,1)} %param.9), channel_id=1, replica_groups=mesh['blk'=32,'src'=2,'layer'=4] {'blk'}, dimensions={0}, use_global_device_ids=true | all-gather | bytes 270336 | tf_op jit(solution)/shard_map/all_gather | solution.py:20
  50.0 41.9 %all-gather.7.cloned.1.call-done = bf16[1,512,4096]{2,1,0:T(8,128)(2,1)} async-done(((bf16[1,16,4096]{2,1,0:T(8,128)(2,1)}), bf16[1,512,4096]{2,1,0:T(8,128)(2,1)}) %all-gather.7.cloned.1.call-update) | async-done | bytes 4194320 | tf_op jit(solution)/shard_map/all_gather | solution.py:22
  91.9 5.8 %fusion = f32[512,512]{1,0:T(8,128)S(1)} fusion(bf16[1,512,4096]{2,1,0:T(8,128)(2,1)} %param.6, bf16[1,512,4096]{2,1,0:T(8,128)(2,1)} %all-gather.7.cloned.1.call-done), kind=kOutput, calls=%fused_computation | convolution fusion | flops 2147483648 | bytes 9437184 | tf_op jit(solution)/shard_map/dot_general | solution.py:10
  97.8 75.3 %all-gather.5.cloned.1.call-done = bf16[1,512,4096]{2,1,0:T(8,128)(2,1)} async-done(((bf16[1,16,4096]{2,1,0:T(8,128)(2,1)}), bf16[1,512,4096]{2,1,0:T(8,128)(2,1)}) %all-gather.5.cloned.1.call-update) | async-done | bytes 4194320 | tf_op jit(solution)/shard_map/all_gather | solution.py:21
  173.0 7.1 %fusion.23 = f32[512,256]{1,0:T(8,128)} fusion(bf16[512,256]{1,0:T(8,128)(2,1)S(1)} %all_gather.11, f32[512,512]{1,0:T(8,128)S(1)} %fusion, bf16[1,512,4096]{2,1,0:T(8,128)(2,1)} %param.5, bf16[1,512,4096]{2,1,0:T(8,128)(2,1)} %all-gather.5.cloned.1.call-done), kind=kOutput, calls=%fused_computation.9 | convolution fusion | flops 2282487808 | bytes 10223616 | tf_op jit(solution)/shard_map/dot_general | solution.py:26
  180.1 0.0 reduce-scatter.2.cloned.1.call-update
  180.1 0.0 all-reduce.2.cloned.1.call-start
  180.2 34.0 %reduce-scatter.2.cloned.1.call-done = f32[128,256]{1,0:T(8,128)} async-done(((f32[512,256]{1,0:T(8,128)}), f32[128,256]{1,0:T(8,128)}) %reduce-scatter.2.cloned.1.call-update) | async-done | bytes 131088 | tf_op jit(solution)/shard_map/reduce_scatter | solution.py:29
  214.2 0.0 all-reduce.2.cloned.1.call-update
  214.2 34.8 %all-reduce.2.cloned.1.call-done = f32[128,256]{1,0:T(8,128)} async-done(((f32[128,256]{1,0:T(8,128)}), f32[128,256]{1,0:T(8,128)}) %all-reduce.2.cloned.1.call-update) | async-done | bytes 131088 | tf_op jit(solution)/shard_map/psum | solution.py:30
  249.0 1.6 broadcast_multiply_fusion
Async XLA Ops:
  6.5 85.4 %all-gather.7.cloned.1.call-start = ((), (), s32[]{:S(2)}) async-start(), calls=%async_computation.4 | async-start | bytes 4325376 | tf_op jit(solution)/shard_map/all_gather | solution.py:22
  7.3 165.8 %all-gather.5.cloned.1.call-start = ((), (), s32[]{:S(2)}) async-start(), calls=%async_computation.3 | async-start | bytes 4325376 | tf_op jit(solution)/shard_map/all_gather | solution.py:21
  8.0 206.1 %reduce-scatter.2.cloned.1.call-start = ((), (), s32[]{:S(2)}) async-start(), calls=%async_computation.1 | async-start | bytes 655360 | tf_op jit(solution)/shard_map/reduce_scatter | solution.py:29
  180.1 68.9 %all-reduce.2.cloned.1.call-start = ((), (), s32[]{:S(2)}) async-start(), calls=%async_computation.2 | async-start | bytes 262144 | tf_op jit(solution)/shard_map/psum | solution.py:30
Sparse Core Ops, SparseCore 0:
  9.9 81.9 all-gather.6
  94.5 78.4 all-gather.4
  180.3 33.8 reduce-scatter.1
  216.6 32.3 all-reduce.1
where the time goes:
time: 257 us
  waiting for transfers between devices  187 us (73%)
  blocking collectives  42 us (16%)
  between operations  13.1 us (5%)
  matrix products  12.9 us (5%)
    all_gather x1, waiting for transfers between devices, on_device(): acts = lax.all_gather(source_act[0], 'blk', axis=0, tiled=True)  75.3 us
    all_gather x1, blocking collectives, on_device(): probe_rows = lax.all_gather(probes, 'blk', axis=0, tiled=True)  42 us
    all_gather x1, waiting for transfers between devices, on_device(): grads = lax.all_gather(source_grad[0], 'blk', axis=0, tiled=True)  41.9 us
    psum x1, waiting for transfers between devices, on_device(): result = lax.psum(part, 'src')  34.8 us
    reduce_scatter x1, waiting for transfers between devices, on_device(): part = lax.psum_scatter(total, 'layer', scatter_dimension=0, tiled=True)  34 us
    dot_general x1, matrix products, on_device(): lax.dot_general(kernel, probe_rows, (((0,), (0,)), ((), ())), preferred_e...  7.07 us
    dot_general x1, matrix products, contract_rows(): lax.dot_general(left, right, (((1,), (1,)), ((), ())), preferred_element_...  5.82 us
  transfers between devices with their start and end apart: 4, of which 4 were waited for; matrix products, arithmetic and copies ran while one was open for 2% of the time, Pallas kernels for 0%

commit v1 on v0

--- a/solution.py
+++ b/solution.py
@@ -4,6 +4,12 @@
 from jax.sharding import PartitionSpec as P
 
 LAYERS = 4
+
+
+def _direct_steps_all(here_x):
+    w2 = lax.all_gather(here_x, axis_name="src")
+    plain = jnp.sum(w2, 0)
+    return plain
 
 
 def contract_rows(left, right):
@@ -27,7 +33,7 @@
         kernel, probe_rows, (((0,), (0,)), ((), ())), preferred_element_type=jnp.float32
     )
     part = lax.psum_scatter(total, "layer", scatter_dimension=0, tiled=True)
-    result = lax.psum(part, "src")
+    result = _direct_steps_all(part)
     return result * jnp.float32((LAYERS * source_total) ** (-0.5))
 
 

time: 257 us -> 227 us (0.88)
  waiting for transfers between devices: 187 us -> 153 us
  blocking collectives: 42 us -> 47.1 us
    psum x1 -> x0, waiting for transfers between devices: 34.8 us -> none  [on_device(): result = lax.psum(part, 'src')]
    all_gather x0 -> x1, blocking collectives: none -> 5.08 us  [_direct_steps_all(): w2 = lax.all_gather(here_x, axis_name='src')]
  transfers between devices with their start and end apart: 4 -> 3, of which waited for: 4 -> 3; matrix products, arithmetic and copies ran while one was open for 2% -> 3% of each run, Pallas kernels for 0% -> 0%
where the time goes in v1:
time: 227 us; the launch traced here: 226 us
  waiting for transfers between devices  153 us (67%)
  blocking collectives  47.1 us (21%)
  between operations  13.1 us (6%)
  matrix products  12.9 us (6%)
    all_gather x1, waiting for transfers between devices, on_device(): acts = lax.all_gather(source_act[0], 'blk', axis=0, tiled=True)  75.3 us
    all_gather x1, blocking collectives, on_device(): probe_rows = lax.all_gather(probes, 'blk', axis=0, tiled=True)  42 us
    all_gather x1, waiting for transfers between devices, on_device(): grads = lax.all_gather(source_grad[0], 'blk', axis=0, tiled=True)  41.9 us
    reduce_scatter x1, waiting for transfers between devices, on_device(): part = lax.psum_scatter(total, 'layer', scatter_dimension=0, tiled=True)  34 us
    dot_general x1, matrix products, on_device(): lax.dot_general(kernel, probe_rows, (((0,), (0,)), ((), ())), preferred_e...  7.07 us
    dot_general x1, matrix products, contract_rows(): lax.dot_general(left, right, (((1,), (1,)), ((), ())), preferred_element_...  5.82 us
    all_gather x1, blocking collectives, _direct_steps_all(): w2 = lax.all_gather(here_x, axis_name='src')  5.08 us
  transfers between devices with their start and end apart: 3, of which 3 were waited for; matrix products, arithmetic and copies ran while one was open for 3% of the time, Pallas kernels for 0%

profile of v1, /device:TPU:1, one launch (start us, length us, event | category | flops | bytes accessed | tf_op | source)
XLA Modules:
  0.0 226.5 jit_solution(6347251749726440744)
XLA Ops:
  6.5 0.0 all-gather.8.cloned.1.call-start
  6.5 0.7 all-gather.8.cloned.1.call-update
  7.3 0.0 all-gather.6.cloned.1.call-start
  7.3 0.7 all-gather.6.cloned.1.call-update
  8.0 0.0 reduce-scatter.2.cloned.1.call-start
  8.1 42.0 %all_gather.17 = bf16[512,256]{1,0:T(8,128)(2,1)S(1)} all-gather(bf16[16,256]{1,0:T(8,128)(2,1)} %param.9), channel_id=1, replica_groups=mesh['blk'=32,'src'=2,'layer'=4] {'blk'}, dimensions={0}, use_global_device_ids=true | all-gather | bytes 270336 | tf_op jit(solution)/shard_map/all_gather | solution.py:26
  50.0 41.9 %all-gather.8.cloned.1.call-done = bf16[1,512,4096]{2,1,0:T(8,128)(2,1)} async-done(((bf16[1,16,4096]{2,1,0:T(8,128)(2,1)}), bf16[1,512,4096]{2,1,0:T(8,128)(2,1)}) %all-gather.8.cloned.1.call-update) | async-done | bytes 4194320 | tf_op jit(solution)/shard_map/all_gather | solution.py:28
  91.9 5.8 %fusion = f32[512,512]{1,0:T(8,128)S(1)} fusion(bf16[1,512,4096]{2,1,0:T(8,128)(2,1)} %param.6, bf16[1,512,4096]{2,1,0:T(8,128)(2,1)} %all-gather.8.cloned.1.call-done), kind=kOutput, calls=%fused_computation | convolution fusion | flops 2147483648 | bytes 9437184 | tf_op jit(solution)/shard_map/dot_general | solution.py:16
  97.8 75.3 %all-gather.6.cloned.1.call-done = bf16[1,512,4096]{2,1,0:T(8,128)(2,1)} async-done(((bf16[1,16,4096]{2,1,0:T(8,128)(2,1)}), bf16[1,512,4096]{2,1,0:T(8,128)(2,1)}) %all-gather.6.cloned.1.call-update) | async-done | bytes 4194320 | tf_op jit(solution)/shard_map/all_gather | solution.py:27
  173.0 7.1 %fusion.23 = f32[512,256]{1,0:T(8,128)} fusion(bf16[512,256]{1,0:T(8,128)(2,1)S(1)} %all_gather.17, f32[512,512]{1,0:T(8,128)S(1)} %fusion, bf16[1,512,4096]{2,1,0:T(8,128)(2,1)} %param.5, bf16[1,512,4096]{2,1,0:T(8,128)(2,1)} %all-gather.6.cloned.1.call-done), kind=kOutput, calls=%fused_computation.9 | convolution fusion | flops 2282487808 | bytes 10223616 | tf_op jit(solution)/shard_map/dot_general | solution.py:32
  180.1 0.0 reduce-scatter.2.cloned.1.call-update
  180.1 34.0 %reduce-scatter.2.cloned.1.call-done = f32[128,256]{1,0:T(8,128)} async-done(((f32[512,256]{1,0:T(8,128)}), f32[128,256]{1,0:T(8,128)}) %reduce-scatter.2.cloned.1.call-update) | async-done | bytes 131088 | tf_op jit(solution)/shard_map/reduce_scatter | solution.py:35
  214.2 5.1 %all-gather.2 = f32[256,256]{1,0:T(8,128)S(1)} all-gather(f32[128,256]{1,0:T(8,128)} %reduce-scatter.2.cloned.1.call-done), channel_id=4, replica_groups=mesh['blk'=32,'src'=2,'layer'=4] {'src'}, dimensions={0}, use_global_device_ids=true | all-gather | bytes 393216 | tf_op jit(solution)/shard_map/all_gather | solution.py:10
  219.3 0.7 broadcast_multiply_fusion
  (1 shorter events, 0.0 us)
Async XLA Ops:
  6.5 85.4 %all-gather.8.cloned.1.call-start = ((), (), s32[]{:S(2)}) async-start(), calls=%async_computation.3 | async-start | bytes 4325376 | tf_op jit(solution)/shard_map/all_gather | solution.py:28
  7.3 165.8 %all-gather.6.cloned.1.call-start = ((), (), s32[]{:S(2)}) async-start(), calls=%async_computation.2 | async-start | bytes 4325376 | tf_op jit(solution)/shard_map/all_gather | solution.py:27
  8.0 206.1 %reduce-scatter.2.cloned.1.call-start = ((), (), s32[]{:S(2)}) async-start(), calls=%async_computation.1 | async-start | bytes 655360 | tf_op jit(solution)/shard_map/reduce_scatter | solution.py:35
Sparse Core Ops, SparseCore 0:
  9.9 81.9 all-gather.7
  94.5 78.4 all-gather.5
  180.3 33.8 reduce-scatter.1
